TPU v7x, 32 devices: a whole 2x2x4 slice. The times are simulated.
32 devices in a mesh: grp: 4 (over y, x), sub: 8 (over z, core).
Axes of the slice: x: 2, y: 2, z: 4, core: 2. Of those that a mesh axis runs over, the one named last changes fastest.
Arguments:
- reg_disp: float32 [4, 8, 3, 384], P('grp', 'sub'), may hold values from -6 to 6
- reg_vel: float32 [4, 8, 3, 384], P('grp', 'sub'), may hold values from -0.6 to 0.6
- site_disp: float32 [4, 8, 3, 1536], P('grp', 'sub'), may hold values from -6 to 6
- site_vel: float32 [4, 8, 3, 1536], P('grp', 'sub'), may hold values from -0.6 to 0.6
- reg_nodes: int32 [4, 8, 10, 256], P('grp', 'sub'), may hold values from 0 to 383
- site_nodes: int32 [4, 8, 35, 128], P('grp', 'sub'), may hold values from 0 to 1535
- reg_coefs: float32 [4, 8, 3, 3, 4, 256], P('grp', 'sub'), may hold values from -1.5 to 6, as said below
- site_coefs: float32 [4, 8, 3, 3, 24, 128], P('grp', 'sub'), may hold values from -1.5 to 6, as said below
- reg_table: float32 [12, 10], replicated, may hold values from -2 to 2
- site_table: float32 [72, 35], replicated, may hold values from -1 to 1
- reg_minv: float32 [4, 8, 384], P('grp', 'sub'), may hold values from 0.003 to 0.015
- site_minv: float32 [4, 8, 1536], P('grp', 'sub'), may hold values from 0.003 to 0.015
- reg_send: int32 [4, 8, 2, 128], P('grp', 'sub'), may hold values from 0 to 383
- reg_recv: int32 [4, 8, 2, 128], P('grp', 'sub'), may hold values from 0 to 383
- site_send: int32 [4, 8, 2, 128], P('grp', 'sub'), may hold values from 0 to 1535
- site_recv: int32 [4, 8, 2, 128], P('grp', 'sub'), may hold values from 0 to 1535
- slot_fill: int32 [4, 8, 4], P('grp', 'sub'), may hold values from 1 to 128, 384 in all within a row
- layer_src: int32 [4, 8, 128], P('grp', 'sub'), may hold values from 0 to 383
- layer_fill: int32 [4, 8], P('grp', 'sub'), may hold values from 64 to 128, as said below
- layer_dst: int32 [4, 8, 3, 128], P('grp', 'sub'), may hold values from 0 to 1535
- layer_stiff: float32 [4, 8, 3, 128], P('grp', 'sub'), may hold values from 0.5 to 2
Outputs:
- reg_final: float32 [4, 8, 3, 384], P('grp', 'sub')
- site_final: float32 [4, 8, 3, 1536], P('grp', 'sub')
Inputs may be any that keep to these rules, and one draw needn't show every extreme that they name: `slot_fill`: per partition the four entries count live slots toward the lower and higher neighbour, regional then site; they sum to 384. `layer_fill`: partition index 0 of every group fills all 128 slots. `reg_coefs`: each 3 x 3 tensor over the first two dimensions is symmetric positive definite. `site_coefs`: each 3 x 3 tensor over the first two dimensions is symmetric positive definite.
All inputs are finite; a program needn't handle non-finite values.
Results may differ from a plain program's by a relative error of at most 0.0003.
Values sent between devices are 32-bit elements; how exact they have to be, the bound alone decides.
A program may use at most 64 MiB of HBM per device.

v0:
```python
import jax
import jax.numpy as jnp
from jax import lax
from jax.sharding import PartitionSpec as P

STEPS = 8
MB_STEPS = 2


PRECISE = lax.Precision.HIGHEST


def with_halo(value, sides, width):
    for axis, dim in sides:
        count, length = (lax.axis_size(axis), value.shape[dim])
        up = [(i, (i + 1) % count) for i in range(count - 1)]
        down = [(j, i) for i, j in up]
        last = lax.slice_in_dim(value, length - width, length, axis=dim)
        leading = lax.slice_in_dim(value, 0, width, axis=dim)
        before = lax.ppermute(last, axis, up)
        after = lax.ppermute(leading, axis, down)
        value = jnp.concatenate([before, value, after], axis=dim)
    return value


def shifted(block, axis, distance):
    devices = range(lax.axis_size(axis))
    route = [(i - distance, i) for i in devices if i - distance in devices]
    return lax.ppermute(block, axis, route)


def stiff_force(displaced, element_nodes, coef_block, deriv_table):
    quad_count = coef_block.shape[2]
    node_count = element_nodes.shape[0]
    elem_count = element_nodes.shape[1]
    flat_nodes = element_nodes.reshape(-1)
    gathered = jnp.take(displaced, flat_nodes, axis=1).reshape(3, node_count, elem_count)
    gradient = jnp.einsum("kp,cpe->cke", deriv_table, gathered, precision=PRECISE)
    pieces = [gradient[:, b * quad_count : (b + 1) * quad_count] for b in range(3)]
    flux_rows = [
        coef_block[a, 0][None] * pieces[0]
        + coef_block[a, 1][None] * pieces[1]
        + coef_block[a, 2][None] * pieces[2]
        for a in range(3)
    ]
    flux_terms = jnp.concatenate(flux_rows, axis=1)
    element_terms = jnp.einsum("kp,cke->cpe", deriv_table, flux_terms, precision=PRECISE)
    return -jnp.zeros_like(displaced).at[:, flat_nodes].add(element_terms.reshape(3, -1))


def pack_slots(forces, send_map, fill_pair):
    picked = jnp.take(forces, send_map, axis=1)
    live_slots = jnp.arange(send_map.shape[1], dtype=jnp.int32)[None, :] < fill_pair[:, None]
    return jnp.where(live_slots[:, None, :], jnp.transpose(picked, (1, 0, 2)), 0.0)


def take_slots(forces, recv_map, from_lower, from_upper):
    return forces.at[:, recv_map[0]].add(from_lower).at[:, recv_map[1]].add(from_upper)


def pack_layer(displaced, layer_src, layer_fill):
    picked = jnp.take(displaced, layer_src, axis=1)
    live_slots = jnp.arange(layer_src.shape[0], dtype=jnp.int32) < layer_fill
    return jnp.where(live_slots[None, :], picked, 0.0)


def add_layer(forces, layer_dst, layer_stiff, layer_block):
    for source in range(3):
        forces = forces.at[:, layer_dst[source]].add(
            layer_stiff[source][None, :] * layer_block[source]
        )
    return forces


def shards(
    reg_disp,
    reg_vel,
    site_disp,
    site_vel,
    reg_nodes,
    site_nodes,
    reg_coefs,
    site_coefs,
    reg_table,
    site_table,
    reg_minv,
    site_minv,
    reg_send,
    reg_recv,
    site_send,
    site_recv,
    slot_fill,
    layer_src,
    layer_fill,
    layer_dst,
    layer_stiff,
):
    group_count = lax.axis_size("grp")
    site_groups = group_count // 4
    reg_groups = 3 * site_groups
    grp_index = lax.axis_index("grp")
    is_site = grp_index >= reg_groups
    reg_now = reg_disp[0, 0]
    site_now = site_disp[0, 0]
    slot_counts = slot_fill[0, 0]
    blank_send = jnp.zeros((2, 3, reg_send.shape[-1]), jnp.float32)

    def advance(states, layer_block, reg_on, site_on):
        reg_pair, site_pair = states

        def reg_force():
            forces = stiff_force(reg_pair[1], reg_nodes[0, 0], reg_coefs[0, 0], reg_table)
            return (
                forces,
                jnp.zeros_like(site_pair[1]),
                pack_slots(forces, reg_send[0, 0], slot_counts[0:2]),
            )

        def site_force():
            forces = stiff_force(site_pair[1], site_nodes[0, 0], site_coefs[0, 0], site_table)
            return (
                jnp.zeros_like(reg_pair[1]),
                forces,
                pack_slots(forces, site_send[0, 0], slot_counts[2:4]),
            )

        def no_force():
            return (jnp.zeros_like(reg_pair[1]), jnp.zeros_like(site_pair[1]), blank_send)

        reg_total, site_total, outgoing = lax.cond(
            is_site, site_force if site_on else no_force, reg_force if reg_on else no_force
        )
        incoming = with_halo(outgoing, (("sub", 0),), 1)
        from_lower = incoming[0]
        from_upper = incoming[3]

        def reg_update():
            forces = take_slots(reg_total, reg_recv[0, 0], from_lower, from_upper)
            reg_next = 2.0 * reg_pair[1] - reg_pair[0] + reg_minv[0, 0][None, :] * forces
            return ((reg_pair[1], reg_next), site_pair)

        def site_update():
            forces = take_slots(site_total, site_recv[0, 0], from_lower, from_upper)
            forces = add_layer(forces, layer_dst[0, 0], layer_stiff[0, 0], layer_block)
            site_next = 2.0 * site_pair[1] - site_pair[0] + site_minv[0, 0][None, :] * forces
            return (reg_pair, (site_pair[1], site_next))

        def keep_states():
            return (reg_pair, site_pair)

        return lax.cond(
            is_site, site_update if site_on else keep_states, reg_update if reg_on else keep_states
        )

    states = ((reg_now - reg_vel[0, 0], reg_now), (site_now - site_vel[0, 0], site_now))
    batch_count = STEPS // MB_STEPS
    pending = None
    for batch_no in range(batch_count + 1):
        layer_packs = []
        for inner_step in range(MB_STEPS):
            layer_block = pending[:, inner_step] if batch_no > 0 else None
            states = advance(states, layer_block, batch_no < batch_count, batch_no > 0)
            if batch_no < batch_count:
                layer_packs.append(pack_layer(states[0][1], layer_src[0, 0], layer_fill[0, 0]))
        if batch_no < batch_count:
            layer_steps = jnp.stack(layer_packs)
            pending = jnp.stack(
                [shifted(layer_steps, "grp", (3 - source) * site_groups) for source in range(3)]
            )
    reg_final = jnp.where(is_site, 0.0, states[0][1])[None, None]
    site_final = jnp.where(is_site, states[1][1], 0.0)[None, None]
    return (reg_final, site_final)


def solution(mesh):
    return jax.shard_map(
        shards,
        mesh=mesh,
        in_specs=(
            P("grp", "sub", None, None),
            P("grp", "sub", None, None),
            P("grp", "sub", None, None),
            P("grp", "sub", None, None),
            P("grp", "sub", None, None),
            P("grp", "sub", None, None),
            P("grp", "sub", None, None, None, None),
            P("grp", "sub", None, None, None, None),
            P(),
            P(),
            P("grp", "sub", None),
            P("grp", "sub", None),
            P("grp", "sub", None, None),
            P("grp", "sub", None, None),
            P("grp", "sub", None, None),
            P("grp", "sub", None, None),
            P("grp", "sub", None),
            P("grp", "sub", None),
            P("grp", "sub"),
            P("grp", "sub", None, None),
            P("grp", "sub", None, None),
        ),
        out_specs=(P("grp", "sub", None, None), P("grp", "sub", None, None)),
        check_vma=False,
    )
```

profile of v0, /device:TPU:23, one launch (start us, length us, event | category | flops | bytes accessed | tf_op | source)
XLA Modules:
  0.0 590.9 jit_solution(15146022666100904936)
XLA Ops:
  24.6 47.2 %conditional.24 = (f32[3,384]{0,1:T(8,128)S(1)}, f32[3,1536]{1,0:T(4,128)S(1)}, f32[2,3,128]{1,2,0:T(8,128)}) conditional(s32[]{:T(128)} %convert_element_type.2, (s32[1,1,10,256]{3,1,2,0:T(1,128)S(1)}, f32[1,1,3,3,4,256]{5,4,3,2,1,0:T(4,128)S(1)}, f32[3,384]{0,1:T(8,128)S(1)}, f32[12,10]{1,0:T(8,128)S(1)}, s32[4]{0:T(128)S(1)}, ...), branch_computations={%region_14.18_spmd, %region_16.22_spmd} | conditional | flops 23513344 | bytes 1754184 | solution.py:130
  25.3 9.2 %gather_fusion.6 = f32[4480,3]{1,0:T(8,128)} fusion(f32[3,1536]{0,1:T(8,128)S(1)} %get-tuple-element.568, s32[5120]{0:T(1024)S(1)} %pad_clamp_fusion.6), kind=kCustom, calls=%fused_computation.2.clone | custom fusion | bytes 125440 | tf_op jit(solution)/shard_map/cond/branch_1_fun/jit(_take)/gather | solution.py:37
  44.2 25.6 %scatter_custom_fusion.5 = f32[3,1536]{0,1:T(8,128)S(1)} fusion(s32[4480]{0:T(1024)S(1)} %fusion.289, f32[4480,3]{1,0:T(8,128)} %bitcast.1637, f32[]{:T(128)} %constant.72.clone), kind=kCustom, calls=%fused_computation.562 | custom fusion | flops 13440 | bytes 18944 | tf_op jit(solution)/shard_map/cond/branch_1_fun/scatter-add | solution.py:48
  85.3 12.6 %conditional.25 = (f32[3,384]{1,0:T(4,128)S(1)}, f32[3,384]{1,0:T(4,128)S(1)}, f32[3,1536]{0,1:T(8,128)S(1)}, f32[3,1536]{0,1:T(8,128)S(1)}, f32[3,384]{0,1:T(8,128)S(1)}) conditional(s32[]{:T(128)} %convert_element_type.2, (f32[3,384]{0,1:T(8,128)S(1)}, f32[3,384]{0,1:T(8,128)S(1)}, f32[1,1,384]{2,1,0:T(1,128)S(1)}, ...), branch_computations={%region_18.0_spmd, %region_21.32_spmd} | conditional | flops 23424 | bytes 712264 | solution.py:151
  98.8 47.2 %conditional.26 = (f32[3,384]{0,1:T(8,128)S(1)}, f32[3,1536]{1,0:T(4,128)S(1)}, f32[2,3,128]{1,2,0:T(8,128)}) conditional(s32[]{:T(128)} %convert_element_type.2, (s32[1,1,10,256]{3,1,2,0:T(1,128)S(1)}, f32[1,1,3,3,4,256]{5,4,3,2,1,0:T(4,128)S(1)}, f32[3,384]{1,0:T(4,128)S(1)}, f32[12,10]{1,0:T(8,128)S(1)}, s32[4]{0:T(128)}, ...), branch_computations={%region_27.34_spmd, %region_29.36_spmd} | conditional | flops 23513344 | bytes 1705096 | solution.py:130
  99.5 9.2 %gather_fusion.10 = f32[4480,3]{1,0:T(8,128)} fusion(f32[3,1536]{0,1:T(8,128)S(1)} %get-tuple-element.601, s32[5120]{0:T(1024)S(1)} %pad_clamp_fusion.10), kind=kCustom, calls=%fused_computation.19.clone | custom fusion | bytes 125440 | tf_op jit(solution)/shard_map/cond/branch_1_fun/jit(_take)/gather | solution.py:37
  118.4 25.6 %scatter_custom_fusion.65 = f32[3,1536]{0,1:T(8,128)S(1)} fusion(s32[4480]{0:T(1024)S(1)} %fusion.315, f32[4480,3]{1,0:T(8,128)} %bitcast.1638, f32[]{:T(128)} %constant.104.clone), kind=kCustom, calls=%fused_computation.636 | custom fusion | flops 13440 | bytes 18944 | tf_op jit(solution)/shard_map/cond/branch_1_fun/scatter-add | solution.py:48
  155.6 11.4 %conditional.27 = (f32[3,384]{1,0:T(4,128)S(1)}, f32[3,384]{1,0:T(4,128)S(1)}, f32[3,1536]{0,1:T(8,128)S(1)}, f32[3,1536]{0,1:T(8,128)S(1)}, f32[3,384]{0,1:T(8,128)S(1)}) conditional(s32[]{:T(128)} %convert_element_type.2, (f32[3,384]{1,0:T(4,128)S(1)}, f32[3,384]{1,0:T(4,128)S(1)}, f32[1,1,384]{2,1,0:T(1,128)S(1)}, s32[1,1,2,128]{3,2,1,0:T(2,128)}, ...), branch_computations={%region_31.39_spmd, %region_34.45_spmd} | conditional | flops 23424 | bytes 739940 | solution.py:151
  173.4 44.3 %conditional.28 = (f32[3,384]{0,1:T(8,128)S(1)}, f32[3,1536]{1,0:T(4,128)S(1)}, f32[2,3,128]{1,2,0:T(8,128)}) conditional(s32[]{:T(128)} %convert_element_type.2, (s32[1,1,10,256]{3,1,2,0:T(1,128)S(1)}, f32[1,1,3,3,4,256]{5,4,3,2,1,0:T(4,128)S(1)}, f32[3,384]{1,0:T(4,128)S(1)}, f32[12,10]{1,0:T(8,128)S(1)}, s32[4]{0:T(128)}, ...), branch_computations={%region_40.47_spmd, %region_42.49_spmd} | conditional | flops 23513344 | bytes 1606736 | solution.py:130
  173.5 9.2 %gather_fusion.14 = f32[4480,3]{1,0:T(8,128)} fusion(f32[3,1536]{0,1:T(8,128)S(1)} %get-tuple-element.634, s32[5120]{0:T(1024)S(1)} %pad_clamp_fusion.14), kind=kCustom, calls=%fused_computation.20.clone | custom fusion | bytes 125440 | tf_op jit(solution)/shard_map/cond/branch_1_fun/jit(_take)/gather | solution.py:37
  190.0 25.6 %scatter_custom_fusion.66 = f32[3,1536]{0,1:T(8,128)S(1)} fusion(s32[4480]{0:T(1024)S(1)} %fusion.341, f32[4480,3]{1,0:T(8,128)} %bitcast.1639, f32[]{:T(128)} %constant.128.clone), kind=kCustom, calls=%fused_computation.710 | custom fusion | flops 13440 | bytes 18944 | tf_op jit(solution)/shard_map/cond/branch_1_fun/scatter-add | solution.py:48
  227.4 11.3 %conditional.29 = (f32[3,384]{1,0:T(4,128)S(1)}, f32[3,384]{1,0:T(4,128)S(1)}, f32[3,1536]{0,1:T(8,128)S(1)}, f32[3,1536]{0,1:T(8,128)S(1)}, f32[3,384]{0,1:T(8,128)S(1)}) conditional(s32[]{:T(128)} %convert_element_type.2, (f32[3,384]{1,0:T(4,128)S(1)}, f32[3,384]{1,0:T(4,128)S(1)}, f32[1,1,384]{2,1,0:T(1,128)S(1)}, s32[1,1,2,128]{3,2,1,0:T(2,128)}, ...), branch_computations={%region_44.52_spmd, %region_47.58_spmd} | conditional | flops 23424 | bytes 624284 | solution.py:151
  239.7 44.3 %conditional.30 = (f32[3,384]{0,1:T(8,128)S(1)}, f32[3,1536]{1,0:T(4,128)S(1)}, f32[2,3,128]{1,2,0:T(8,128)}) conditional(s32[]{:T(128)} %convert_element_type.2, (s32[1,1,10,256]{3,1,2,0:T(1,128)S(1)}, f32[1,1,3,3,4,256]{5,4,3,2,1,0:T(4,128)S(1)}, f32[3,384]{1,0:T(4,128)S(1)}, f32[12,10]{1,0:T(8,128)S(1)}, s32[4]{0:T(128)}, ...), branch_computations={%region_53.60_spmd, %region_55.62_spmd} | conditional | flops 23513344 | bytes 1606736 | solution.py:130
  239.8 9.2 %gather_fusion.18 = f32[4480,3]{1,0:T(8,128)} fusion(f32[3,1536]{0,1:T(8,128)S(1)} %get-tuple-element.667, s32[5120]{0:T(1024)S(1)} %pad_clamp_fusion.18), kind=kCustom, calls=%fused_computation.21.clone | custom fusion | bytes 125440 | tf_op jit(solution)/shard_map/cond/branch_1_fun/jit(_take)/gather | solution.py:37
  256.3 25.6 %scatter_custom_fusion.67 = f32[3,1536]{0,1:T(8,128)S(1)} fusion(s32[4480]{0:T(1024)S(1)} %fusion.367, f32[4480,3]{1,0:T(8,128)} %bitcast.1640, f32[]{:T(128)} %constant.152.clone), kind=kCustom, calls=%fused_computation.784 | custom fusion | flops 13440 | bytes 18944 | tf_op jit(solution)/shard_map/cond/branch_1_fun/scatter-add | solution.py:48
  292.4 11.4 %conditional.31 = (f32[3,384]{1,0:T(4,128)S(1)}, f32[3,384]{1,0:T(4,128)S(1)}, f32[3,1536]{0,1:T(8,128)S(1)}, f32[3,1536]{0,1:T(8,128)S(1)}, f32[3,384]{0,1:T(8,128)S(1)}) conditional(s32[]{:T(128)} %convert_element_type.2, (f32[3,384]{1,0:T(4,128)S(1)}, f32[3,384]{1,0:T(4,128)S(1)}, f32[1,1,384]{2,1,0:T(1,128)S(1)}, s32[1,1,2,128]{3,2,1,0:T(2,128)}, ...), branch_computations={%region_57.65_spmd, %region_60.71_spmd} | conditional | flops 23424 | bytes 739940 | solution.py:151
  310.2 44.3 %conditional.32 = (f32[3,384]{0,1:T(8,128)S(1)}, f32[3,1536]{1,0:T(4,128)S(1)}, f32[2,3,128]{1,2,0:T(8,128)}) conditional(s32[]{:T(128)} %convert_element_type.2, (s32[1,1,10,256]{3,1,2,0:T(1,128)S(1)}, f32[1,1,3,3,4,256]{5,4,3,2,1,0:T(4,128)S(1)}, f32[3,384]{1,0:T(4,128)S(1)}, f32[12,10]{1,0:T(8,128)S(1)}, s32[4]{0:T(128)}, ...), branch_computations={%region_66.73_spmd, %region_68.75_spmd} | conditional | flops 23513344 | bytes 1606736 | solution.py:130
  310.3 9.2 %gather_fusion.22 = f32[4480,3]{1,0:T(8,128)} fusion(f32[3,1536]{0,1:T(8,128)S(1)} %get-tuple-element.700, s32[5120]{0:T(1024)S(1)} %pad_clamp_fusion.22), kind=kCustom, calls=%fused_computation.22.clone | custom fusion | bytes 125440 | tf_op jit(solution)/shard_map/cond/branch_1_fun/jit(_take)/gather | solution.py:37
  326.8 25.6 %scatter_custom_fusion.68 = f32[3,1536]{0,1:T(8,128)S(1)} fusion(s32[4480]{0:T(1024)S(1)} %fusion.393, f32[4480,3]{1,0:T(8,128)} %bitcast.1641, f32[]{:T(128)} %constant.176.clone), kind=kCustom, calls=%fused_computation.858 | custom fusion | flops 13440 | bytes 18944 | tf_op jit(solution)/shard_map/cond/branch_1_fun/scatter-add | solution.py:48
  364.6 10.7 %conditional.33 = (f32[3,384]{1,0:T(4,128)S(1)}, f32[3,384]{1,0:T(4,128)S(1)}, f32[3,1536]{0,1:T(8,128)S(1)}, f32[3,1536]{0,1:T(8,128)S(1)}, f32[3,384]{0,1:T(8,128)S(1)}) conditional(s32[]{:T(128)} %convert_element_type.2, (f32[3,384]{1,0:T(4,128)S(1)}, f32[3,384]{1,0:T(4,128)S(1)}, f32[1,1,384]{2,1,0:T(1,128)S(1)}, s32[1,1,2,128]{3,2,1,0:T(2,128)}, ...), branch_computations={%region_70.78_spmd, %region_73.84_spmd} | conditional | flops 23424 | bytes 739940 | solution.py:151
  376.2 44.3 %conditional.34 = (f32[3,384]{0,1:T(8,128)S(1)}, f32[3,1536]{1,0:T(4,128)S(1)}, f32[2,3,128]{1,2,0:T(8,128)}) conditional(s32[]{:T(128)} %convert_element_type.2, (s32[1,1,10,256]{3,1,2,0:T(1,128)S(1)}, f32[1,1,3,3,4,256]{5,4,3,2,1,0:T(4,128)S(1)}, f32[3,384]{1,0:T(4,128)S(1)}, f32[12,10]{1,0:T(8,128)S(1)}, s32[4]{0:T(128)}, ...), branch_computations={%region_79.86_spmd, %region_81.88_spmd} | conditional | flops 23513344 | bytes 1606736 | solution.py:130
  376.3 9.2 %gather_fusion.26 = f32[4480,3]{1,0:T(8,128)} fusion(f32[3,1536]{0,1:T(8,128)S(1)} %get-tuple-element.733, s32[5120]{0:T(1024)S(1)} %pad_clamp_fusion.26), kind=kCustom, calls=%fused_computation.23.clone | custom fusion | bytes 125440 | tf_op jit(solution)/shard_map/cond/branch_1_fun/jit(_take)/gather | solution.py:37
  392.9 25.6 %scatter_custom_fusion.69 = f32[3,1536]{0,1:T(8,128)S(1)} fusion(s32[4480]{0:T(1024)S(1)} %fusion.419, f32[4480,3]{1,0:T(8,128)} %bitcast.1642, f32[]{:T(128)} %constant.200.clone), kind=kCustom, calls=%fused_computation.932 | custom fusion | flops 13440 | bytes 18944 | tf_op jit(solution)/shard_map/cond/branch_1_fun/scatter-add | solution.py:48
  429.0 10.5 %conditional.35 = (f32[3,384]{1,0:T(4,128)S(1)}, f32[3,1536]{0,1:T(8,128)S(1)}, f32[3,1536]{0,1:T(8,128)S(1)}, f32[3,384]{0,1:T(8,128)S(1)}) conditional(s32[]{:T(128)} %convert_element_type.2, (f32[3,384]{1,0:T(4,128)S(1)}, f32[3,384]{1,0:T(4,128)S(1)}, f32[1,1,384]{2,1,0:T(1,128)S(1)}, s32[1,1,2,128]{3,2,1,0:T(2,128)}, f32[3,384]{0,1:T(8,128)S(1)}, ...), branch_computations={%region_83.91_spmd, %region_86.97_spmd} | conditional | flops 23424 | bytes 739932 | solution.py:151
  445.9 45.4 %conditional.36 = (f32[3,1536]{0,1:T(8,128)}, f32[2,3,128]{1,2,0:T(8,128)S(1)}) conditional(s32[]{:T(128)} %convert_element_type.2, () %tuple.204, (s32[1,1,35,128]{3,1,2,0:T(1,128)S(1)}, f32[1,1,3,3,24,128]{5,4,3,2,1,0:T(8,128)S(1)}, f32[3,1536]{0,1:T(8,128)S(1)}, f32[72,35]{0,1:T(8,128)S(1)}, s32[4]{0:T(128)S(1)}, ...), branch_computations={%region_92.98_spmd, %region_93.100_spmd} | conditional | flops 23513344 | bytes 1565160 | solution.py:130
  446.0 9.2 %gather_fusion.28 = f32[4480,3]{1,0:T(8,128)} fusion(f32[3,1536]{0,1:T(8,128)S(1)} %get-tuple-element.759, s32[5120]{0:T(1024)S(1)} %pad_clamp_fusion.28), kind=kCustom, calls=%fused_computation.24.clone | custom fusion | bytes 125440 | tf_op jit(solution)/shard_map/cond/branch_1_fun/jit(_take)/gather | solution.py:37
  462.5 25.6 %scatter_custom_fusion.70 = f32[3,1536]{0,1:T(8,128)S(1)} fusion(s32[4480]{0:T(1024)S(1)} %fusion.432, f32[4480,3]{1,0:T(8,128)} %bitcast.1635, f32[]{:T(128)} %constant.209.clone), kind=kCustom, calls=%fused_computation.969 | custom fusion | flops 13440 | bytes 18944 | tf_op jit(solution)/shard_map/cond/branch_1_fun/scatter-add | solution.py:48
  499.2 17.9 %conditional.37 = (f32[3,1536]{0,1:T(8,128)S(1)}, f32[3,1536]{0,1:T(8,128)S(1)}) conditional(s32[]{:T(128)} %convert_element_type.2, (f32[3,1536]{0,1:T(8,128)}, f32[3,1536]{0,1:T(8,128)S(1)}) %tuple.663, (f32[3,1536]{0,1:T(8,128)S(1)}, f32[3,1536]{0,1:T(8,128)}, f32[1,1,1536]{2,1,0:T(1,128)S(1)}, s32[1,1,2,128]{3,2,1,0:T(2,128)S(1)}, ...), branch_computations={%region_95.101_spmd.clone, %region_96.0_spmd.clone} | conditional | flops 23424 | bytes 656944 | solution.py:151
  518.0 46.0 %conditional.38 = (f32[3,1536]{0,1:T(8,128)}, f32[2,3,128]{1,2,0:T(8,128)S(1)}) conditional(s32[]{:T(128)} %convert_element_type.2, () %tuple.207, (s32[1,1,35,128]{3,1,2,0:T(1,128)S(1)}, f32[1,1,3,3,24,128]{5,4,3,2,1,0:T(8,128)S(1)}, f32[3,1536]{0,1:T(8,128)S(1)}, f32[72,35]{0,1:T(8,128)S(1)}, s32[4]{0:T(128)S(1)}, ...), branch_computations={%region_102.108_spmd, %region_103.110_spmd} | conditional | flops 23513344 | bytes 1565160 | solution.py:130
  518.3 9.2 %gather_fusion.30 = f32[4480,3]{1,0:T(8,128)} fusion(f32[3,1536]{0,1:T(8,128)S(1)} %get-tuple-element.777, s32[5120]{0:T(1024)S(1)} %pad_clamp_fusion.30), kind=kCustom, calls=%fused_computation.25.clone | custom fusion | bytes 125440 | tf_op jit(solution)/shard_map/cond/branch_1_fun/jit(_take)/gather | solution.py:37
  534.9 25.6 %scatter_custom_fusion.71 = f32[3,1536]{0,1:T(8,128)S(1)} fusion(s32[4480]{0:T(1024)S(1)} %fusion.445, f32[4480,3]{1,0:T(8,128)} %bitcast.1636, f32[]{:T(128)} %constant.223.clone), kind=kCustom, calls=%fused_computation.1006 | custom fusion | flops 13440 | bytes 18944 | tf_op jit(solution)/shard_map/cond/branch_1_fun/scatter-add | solution.py:48
  571.5 18.2 %conditional.39 = (f32[3,1536]{1,0:T(4,128)S(1)}) conditional(s32[]{:T(128)} %convert_element_type.2, f32[3,1536]{0,1:T(8,128)S(1)} %get-tuple-element.900, (f32[3,1536]{0,1:T(8,128)S(1)}, f32[3,1536]{0,1:T(8,128)}, f32[1,1,1536]{2,1,0:T(1,128)S(1)}, s32[1,1,2,128]{3,2,1,0:T(2,128)S(1)}, f32[3,1536]{0,1:T(8,128)}, ...), branch_computations={%region_105.111_spmd, %region_106.0_spmd} | conditional | flops 23424 | bytes 656936 | solution.py:151
  (534 shorter events, 303.4 us)
Async XLA Ops:
  1.7 7.2 %collective-permute-start = (f32[1,3,128]{1,2,0:T(8,128)S(1)}, f32[1,3,128]{1,2,0:T(8,128)S(1)}, u32[]{:S(2)}, u32[]{:S(2)}) collective-permute-start(f32[1,3,128]{1,2,0:T(8,128)S(1)} %get-tuple-element.2092), channel_id=1, source_target_pairs={{0,1},{1,2},{2,3},{3,4},{4,5},{5,6},{6,7},{8,9},{9,10},{10,11},{11... | collective-permute-start | bytes 4616 | tf_op jit(solution)/shard_map/ppermute | solution.py:20
  5.4 5.6 collective-permute-start.1
  11.3 6.7 %collective-permute-start.2 = (f32[1,3,128]{1,2,0:T(8,128)S(1)}, f32[1,3,128]{1,2,0:T(8,128)S(1)}, u32[]{:S(2)}, u32[]{:S(2)}) collective-permute-start(f32[1,3,128]{1,2,0:T(8,128)S(1)} %get-tuple-element.2090), channel_id=1, source_target_pairs={{0,1},{1,2},{2,3},{3,4},{4,5},{5,6},{6,7},{8,9},{9,10},{10,11},{11... | collective-permute-start | bytes 4616 | tf_op jit(solution)/shard_map/ppermute | solution.py:20
  13.3 5.6 collective-permute-start.3
  20.7 60.1 %collective-permute-start.6 = (f32[2,3,128]{2,0,1:T(2,128)}, f32[2,3,128]{2,0,1:T(2,128)}, u32[]{:S(2)}, u32[]{:S(2)}) collective-permute-start(f32[2,3,128]{2,0,1:T(2,128)} %pad_maximum_fusion.4), channel_id=1, source_target_pairs={{0,24},{1,25},{2,26},{3,27},{4,28},{5,29},{6,30},{7,31}} | collective-permute-start | bytes 9224 | tf_op jit(solution)/shard_map/ppermute | solution.py:29
  22.0 60.1 %collective-permute-start.7 = (f32[2,3,128]{2,0,1:T(2,128)}, f32[2,3,128]{2,0,1:T(2,128)}, u32[]{:S(2)}, u32[]{:S(2)}) collective-permute-start(f32[2,3,128]{2,0,1:T(2,128)} %pad_maximum_fusion.4), channel_id=1, source_target_pairs={{0,16},{8,24},{1,17},{9,25},{2,18},{10,26},{3,19},{11,27},{4,20},{... | collective-permute-start | bytes 9224 | tf_op jit(solution)/shard_map/ppermute | solution.py:29
  23.3 60.7 %collective-permute-start.8 = (f32[2,3,128]{2,0,1:T(2,128)}, f32[2,3,128]{2,0,1:T(2,128)}, u32[]{:S(2)}, u32[]{:S(2)}) collective-permute-start(f32[2,3,128]{2,0,1:T(2,128)} %pad_maximum_fusion.4), channel_id=1, source_target_pairs={{0,8},{8,16},{16,24},{1,9},{9,17},{17,25},{2,10},{10,18},{18,26},{... | collective-permute-start | bytes 9224 | tf_op jit(solution)/shard_map/ppermute | solution.py:29
  72.9 5.6 collective-permute-start.4
  75.1 5.6 collective-permute-start.5
  146.9 6.4 %collective-permute-start.9 = (f32[1,3,128]{1,2,0:T(8,128)S(1)}, f32[1,3,128]{1,2,0:T(8,128)S(1)}, u32[]{:S(2)}, u32[]{:S(2)}) collective-permute-start(f32[1,3,128]{1,2,0:T(8,128)S(1)} %get-tuple-element.2086), channel_id=1, source_target_pairs={{0,1},{1,2},{2,3},{3,4},{4,5},{5,6},{6,7},{8,9},{9,10},{10,11},{11... | collective-permute-start | bytes 4616 | tf_op jit(solution)/shard_map/ppermute | solution.py:20
  150.0 5.6 collective-permute-start.10
  169.5 56.6 %collective-permute-start.13 = (f32[2,3,128]{2,0,1:T(2,128)}, f32[2,3,128]{2,0,1:T(2,128)}, u32[]{:S(2)}, u32[]{:S(2)}) collective-permute-start(f32[2,3,128]{2,0,1:T(2,128)} %pad_maximum_fusion.5), channel_id=1, source_target_pairs={{0,24},{1,25},{2,26},{3,27},{4,28},{5,29},{6,30},{7,31}} | collective-permute-start | bytes 9224 | tf_op jit(solution)/shard_map/ppermute | solution.py:29
  170.8 55.4 %collective-permute-start.14 = (f32[2,3,128]{2,0,1:T(2,128)}, f32[2,3,128]{2,0,1:T(2,128)}, u32[]{:S(2)}, u32[]{:S(2)}) collective-permute-start(f32[2,3,128]{2,0,1:T(2,128)} %pad_maximum_fusion.5), channel_id=1, source_target_pairs={{0,16},{8,24},{1,17},{9,25},{2,18},{10,26},{3,19},{11,27},{4,20},{... | collective-permute-start | bytes 9224 | tf_op jit(solution)/shard_map/ppermute | solution.py:29
  172.1 54.1 %collective-permute-start.15 = (f32[2,3,128]{2,0,1:T(2,128)}, f32[2,3,128]{2,0,1:T(2,128)}, u32[]{:S(2)}, u32[]{:S(2)}) collective-permute-start(f32[2,3,128]{2,0,1:T(2,128)} %pad_maximum_fusion.5), channel_id=1, source_target_pairs={{0,8},{8,16},{16,24},{1,9},{9,17},{17,25},{2,10},{10,18},{18,26},{... | collective-permute-start | bytes 9224 | tf_op jit(solution)/shard_map/ppermute | solution.py:29
  218.6 4.3 collective-permute-start.11
  220.6 5.6 collective-permute-start.12
  284.9 6.6 %collective-permute-start.16 = (f32[1,3,128]{1,2,0:T(8,128)S(1)}, f32[1,3,128]{1,2,0:T(8,128)S(1)}, u32[]{:S(2)}, u32[]{:S(2)}) collective-permute-start(f32[1,3,128]{1,2,0:T(8,128)S(1)} %get-tuple-element.2082), channel_id=1, source_target_pairs={{0,1},{1,2},{2,3},{3,4},{4,5},{5,6},{6,7},{8,9},{9,10},{10,11},{11... | collective-permute-start | bytes 4616 | tf_op jit(solution)/shard_map/ppermute | solution.py:20
  286.8 5.6 collective-permute-start.17
  306.3 57.0 %collective-permute-start.20 = (f32[2,3,128]{2,0,1:T(2,128)}, f32[2,3,128]{2,0,1:T(2,128)}, u32[]{:S(2)}, u32[]{:S(2)}) collective-permute-start(f32[2,3,128]{2,0,1:T(2,128)} %pad_maximum_fusion.6), channel_id=1, source_target_pairs={{0,24},{1,25},{2,26},{3,27},{4,28},{5,29},{6,30},{7,31}} | collective-permute-start | bytes 9224 | tf_op jit(solution)/shard_map/ppermute | solution.py:29
  307.6 55.7 %collective-permute-start.21 = (f32[2,3,128]{2,0,1:T(2,128)}, f32[2,3,128]{2,0,1:T(2,128)}, u32[]{:S(2)}, u32[]{:S(2)}) collective-permute-start(f32[2,3,128]{2,0,1:T(2,128)} %pad_maximum_fusion.6), channel_id=1, source_target_pairs={{0,16},{8,24},{1,17},{9,25},{2,18},{10,26},{3,19},{11,27},{4,20},{... | collective-permute-start | bytes 9224 | tf_op jit(solution)/shard_map/ppermute | solution.py:29
  308.9 54.4 %collective-permute-start.22 = (f32[2,3,128]{2,0,1:T(2,128)}, f32[2,3,128]{2,0,1:T(2,128)}, u32[]{:S(2)}, u32[]{:S(2)}) collective-permute-start(f32[2,3,128]{2,0,1:T(2,128)} %pad_maximum_fusion.6), channel_id=1, source_target_pairs={{0,8},{8,16},{16,24},{1,9},{9,17},{17,25},{2,10},{10,18},{18,26},{... | collective-permute-start | bytes 9224 | tf_op jit(solution)/shard_map/ppermute | solution.py:29
  355.4 4.3 collective-permute-start.18
  357.7 5.6 collective-permute-start.19
  421.5 6.6 %collective-permute-start.23 = (f32[1,3,128]{1,2,0:T(8,128)S(1)}, f32[1,3,128]{1,2,0:T(8,128)S(1)}, u32[]{:S(2)}, u32[]{:S(2)}) collective-permute-start(f32[1,3,128]{1,2,0:T(8,128)S(1)} %get-tuple-element.2078), channel_id=1, source_target_pairs={{0,1},{1,2},{2,3},{3,4},{4,5},{5,6},{6,7},{8,9},{9,10},{10,11},{11... | collective-permute-start | bytes 4616 | tf_op jit(solution)/shard_map/ppermute | solution.py:20
  423.4 5.6 collective-permute-start.24
  442.0 53.7 %collective-permute-start.27 = (f32[2,3,128]{2,0,1:T(2,128)}, f32[2,3,128]{2,0,1:T(2,128)S(1)}, u32[]{:S(2)}, u32[]{:S(2)}) collective-permute-start(f32[2,3,128]{2,0,1:T(2,128)} %pad_maximum_fusion.7), channel_id=1, source_target_pairs={{0,24},{1,25},{2,26},{3,27},{4,28},{5,29},{6,30},{7,31}} | collective-permute-start | bytes 9224 | tf_op jit(solution)/shard_map/ppermute | solution.py:29
  443.3 52.4 %collective-permute-start.28 = (f32[2,3,128]{2,0,1:T(2,128)}, f32[2,3,128]{2,0,1:T(2,128)}, u32[]{:S(2)}, u32[]{:S(2)}) collective-permute-start(f32[2,3,128]{2,0,1:T(2,128)} %pad_maximum_fusion.7), channel_id=1, source_target_pairs={{0,16},{8,24},{1,17},{9,25},{2,18},{10,26},{3,19},{11,27},{4,20},{... | collective-permute-start | bytes 9224 | tf_op jit(solution)/shard_map/ppermute | solution.py:29
  444.6 51.1 %collective-permute-start.29 = (f32[2,3,128]{2,0,1:T(2,128)}, f32[2,3,128]{2,0,1:T(2,128)}, u32[]{:S(2)}, u32[]{:S(2)}) collective-permute-start(f32[2,3,128]{2,0,1:T(2,128)} %pad_maximum_fusion.7), channel_id=1, source_target_pairs={{0,8},{8,16},{16,24},{1,9},{9,17},{17,25},{2,10},{10,18},{18,26},{... | collective-permute-start | bytes 9224 | tf_op jit(solution)/shard_map/ppermute | solution.py:29
  491.3 5.1 collective-permute-start.25
  493.6 5.6 collective-permute-start.26
  564.0 5.0 collective-permute-start.30
  565.9 5.6 collective-permute-start.31
  (64 other events, 623.0 us)
where the time goes:
time: 603 us; the launch traced here: 591 us
  other arithmetic  351 us (58%)
  local copies, waits for them, and re-layouts  139 us (23%)
  starting transfers between devices  60.9 us (10%)
  waiting for transfers between devices  24.9 us (4%)
    scatter-add x8, other arithmetic, stiff_force(): jnp.zeros_like(displaced).at[:, flat_nodes]  205 us
    gather x8, local copies, waits for them, and re-layouts, stiff_force(): jnp.take(displaced, flat_nodes, axis=1).reshape(3, node_count, elem_count)  73.9 us
    scatter-add x24, other arithmetic, add_layer(): forces.at[:, layer_dst[source]]  48.8 us
    scatter-add x16, other arithmetic, take_slots(): forces.at[:, recv_map[0]].add(from_lower).at[:, recv_map[1]].add(from_upper)  34 us
    select_n x16, other arithmetic, stiff_force(): jnp.take(displaced, flat_nodes, axis=1).reshape(3, node_count, elem_count)  30.3 us
    ppermute x10, starting transfers between devices, with_halo(): before = lax.ppermute(last, axis, up)  23.4 us
    ppermute x10, starting transfers between devices, with_halo(): after = lax.ppermute(leading, axis, down)  22 us
    ppermute x10, waiting for transfers between devices, with_halo(): after = lax.ppermute(leading, axis, down)  21.6 us
  transfers between devices with their start and end apart: 32, of which 13 were waited for; matrix products, arithmetic and copies ran while one was open for 33% of the time, Pallas kernels for 0%

commit v1 on v0

v1 whole, which is shorter than its diff:
```python
import functools

import jax
import jax.numpy as jnp
from jax import lax
from jax.experimental import pallas as pl
from jax.experimental.pallas import tpu as pltpu
from jax.sharding import PartitionSpec as P

STEPS = 8
LANES = 128
MESH = pl.DeviceIdType.MESH
F32 = jnp.float32
BF16 = jnp.bfloat16


def up(size, unit):
    return -(-size // unit) * unit


def lane_gather(block, index):
    numbers = lax.GatherDimensionNumbers(
        offset_dims=(),
        collapsed_slice_dims=(1,),
        start_index_map=(1,),
        operand_batching_dims=(0,),
        start_indices_batching_dims=(0,),
    )
    return lax.gather(
        block,
        index[..., None],
        numbers,
        slice_sizes=(1, 1),
        mode=lax.GatherScatterMode.PROMISE_IN_BOUNDS,
    )


def split(value):
    high = value.astype(BF16)
    low = (value - high.astype(F32)).astype(BF16)
    return high, low


def dot(left, right):
    return jnp.dot(left, right, preferred_element_type=F32)


def spread(rows, blocks, row_block):
    lanes = rows[0].shape[1]
    mine = lax.broadcasted_iota(jnp.int32, (row_block, lanes), 0) == blocks
    return jnp.concatenate([jnp.where(mine, row, 0.0) for row in rows], axis=0).astype(BF16)


def spread_block(block, blocks, row_block):
    high = block.astype(BF16).astype(F32)
    low = block - high
    rows = [part[c : c + 1] for part in (high, low) for c in range(3)]
    return spread(rows, blocks, row_block)


def fill_onehot(out_ref, first_row, lanes_index, tmp_ref):
    count, length = lanes_index.shape
    tmp_ref[...] = jnp.zeros_like(tmp_ref)
    tmp_ref[0:count, :] = lanes_index.astype(F32)
    columns = tmp_ref[...].T
    lane = lax.broadcasted_iota(jnp.int32, (length, LANES), 1).astype(F32)
    for r in range(count):
        hot = jnp.where(lane == columns[:, r : r + 1], 1.0, 0.0)
        out_ref[first_row + r * length : first_row + (r + 1) * length, :] = hot.astype(BF16)


def pick(field, lanes_index, blocks, row_block):
    slots = lanes_index.shape[1]
    index = jnp.broadcast_to(lanes_index, (row_block, slots))
    mine = lax.broadcasted_iota(jnp.int32, (row_block, slots), 0) == blocks
    out = []
    for c in range(3):
        got = lane_gather(field[c * row_block : (c + 1) * row_block], index)
        out.append(jnp.sum(jnp.where(mine, got, 0.0), axis=0, keepdims=True))
    return out


def sizes(nodes_shape, coefs_shape, disp_shape):
    p, e = nodes_shape
    q = coefs_shape[-2]
    h = disp_shape[-1] // LANES
    qp = up(q, 8)
    return dict(p=p, e=e, q=q, h=h, hp=up(h, 8), qp=qp, p8=up(p, 8), pp=up(p, 16), kp=up(3 * qp, 16))


def role_scratch(d, extra_rows):
    return [
        pltpu.VMEM((d["p8"], d["e"]), jnp.int32),
        pltpu.VMEM((d["p8"], d["e"]), jnp.int32),
        pltpu.VMEM((d["p"] * d["e"], LANES), BF16),
        pltpu.VMEM((extra_rows * LANES, LANES), BF16),
        pltpu.VMEM((6 * d["hp"], d["p"] * d["e"]), BF16),
        pltpu.VMEM((2, d["pp"], 3 * d["e"]), F32),
        pltpu.VMEM((9, d["qp"], d["e"]), F32),
        pltpu.VMEM((2 * d["kp"], d["pp"]), BF16),
        pltpu.VMEM((2 * d["pp"], d["kp"]), BF16),
        pltpu.VMEM((3 * d["hp"], LANES), F32),
        pltpu.VMEM((3 * d["hp"], LANES), F32),
        pltpu.VMEM((3 * d["hp"], LANES), F32),
        pltpu.VMEM((LANES, d["e"]), F32),
    ]


def prepare(d, s, disp, vel, nodes, coefs, table, minv, slot_rows, square, tmp):
    (lane_ref, block_ref, hot_ref, slot_hot_ref, _, _, coef_ref, dd_ref, dt_ref, u_ref, prev_ref, minv_ref, tp) = s
    p, q, qp, kp, pp, hp = d["p"], d["q"], d["qp"], d["kp"], d["pp"], d["hp"]
    lane_ref[...] = jnp.zeros_like(lane_ref)
    block_ref[...] = jnp.full_like(block_ref, -1)
    lane_ref[0:p, :] = nodes[...] & (LANES - 1)
    block_ref[0:p, :] = nodes[...] >> 7
    fill_onehot(hot_ref, 0, nodes[...] & (LANES - 1), tp)
    row = 0
    for index in slot_rows:
        fill_onehot(slot_hot_ref, row, index & (LANES - 1), tmp)
        row += index.shape[0] * index.shape[1]
    if qp != q:
        coef_ref[...] = jnp.zeros_like(coef_ref)
    coef_ref[:, 0:q, :] = coefs[...]
    square[...] = jnp.zeros_like(square)
    for b in range(3):
        square[b * qp : b * qp + q, 0:p] = table[b * q : (b + 1) * q, :]
    high, low = split(square[0:kp, 0:pp])
    dd_ref[0:kp, :] = high
    dd_ref[kp : 2 * kp, :] = low
    turned = square[...].T
    square[...] = -turned
    high, low = split(square[0:pp, 0:kp])
    dt_ref[0:pp, :] = high
    dt_ref[pp : 2 * pp, :] = low
    for ref in (u_ref, prev_ref, minv_ref):
        ref[...] = jnp.zeros_like(ref)
    for c in range(3):
        for h in range(d["h"]):
            at, cut = c * hp + h, slice(h * LANES, (h + 1) * LANES)
            now = disp[c : c + 1, cut]
            u_ref[at : at + 1, :] = now
            prev_ref[at : at + 1, :] = now - vel[c : c + 1, cut]
            minv_ref[at : at + 1, :] = minv[0, :, cut]


def element_forces(d, s):
    (lane_ref, block_ref, hot_ref, _, left_ref, fe_ref, coef_ref, dd_ref, dt_ref, u_ref, _, _, _) = s
    p, e, qp, kp, pp, p8, hp = d["p"], d["e"], d["qp"], d["kp"], d["pp"], d["p8"], d["hp"]
    tiles = e // LANES
    got = [[jnp.zeros((p8, LANES), F32) for _ in range(tiles)] for _ in range(3)]
    for t in range(tiles):
        cut = slice(t * LANES, (t + 1) * LANES)
        lanes_index, blocks = lane_ref[:, cut], block_ref[:, cut]
        for h in range(d["h"]):
            mine = blocks == h
            for c in range(3):
                row = jnp.broadcast_to(u_ref[c * hp + h : c * hp + h + 1, :], (p8, LANES))
                got[c][t] = jnp.where(mine, lane_gather(row, lanes_index), got[c][t])
    nodal = jnp.concatenate([got[c][t] for c in range(3) for t in range(tiles)], axis=1)
    if pp != p8:
        nodal = jnp.concatenate([nodal, jnp.zeros((pp - p8, 3 * e), F32)], axis=0)
    high, low = split(nodal)
    both = dot(dd_ref[...], high)
    grad = both[0:kp] + both[kp:] + dot(dd_ref[0:kp, :], low)
    fluxes = []
    for c in range(3):
        cut = slice(c * e, (c + 1) * e)
        pieces = [grad[b * qp : (b + 1) * qp, cut] for b in range(3)]
        rows = [
            coef_ref[3 * a] * pieces[0] + coef_ref[3 * a + 1] * pieces[1] + coef_ref[3 * a + 2] * pieces[2]
            for a in range(3)
        ]
        if kp != 3 * qp:
            rows.append(jnp.zeros((kp - 3 * qp, e), F32))
        fluxes.append(jnp.concatenate(rows, axis=0))
    high, low = split(jnp.concatenate(fluxes, axis=1))
    both = dot(dt_ref[...], high)
    force = both[0:pp] + both[pp:] + dot(dt_ref[0:pp, :], low)
    high = force.astype(BF16).astype(F32)
    fe_ref[0] = high
    fe_ref[1] = force - high
    for n in range(p):
        rows = [fe_ref[k, n : n + 1, c * e : (c + 1) * e] for k in range(2) for c in range(3)]
        left_ref[:, n * e : (n + 1) * e] = spread(rows, block_ref[n : n + 1, :], hp)
    total = dot(left_ref[...], hot_ref[...])
    return total[0 : 3 * hp] + total[3 * hp :]


def kernel(
    n_grp, n_sub, rd, sd,
    reg_disp, reg_vel, site_disp, site_vel, reg_nodes, site_nodes, reg_coefs, site_coefs,
    reg_table, site_table, reg_minv, site_minv, reg_send, reg_recv, site_send, site_recv,
    slot_fill, layer_src, layer_fill, layer_dst, layer_stiff,
    reg_out, site_out,
    send_ref, recv_ref, layer_send_ref, layer_recv_ref, square, tmp,
    halo_send, halo_recv, layer_send, layer_recv,
    *scratch,
):
    half = len(scratch) // 2
    rs, ss = scratch[:half], scratch[half:]
    slots = reg_send.shape[1]
    sites = n_grp // 4
    regs = 3 * sites
    grp, sub = lax.axis_index("grp"), lax.axis_index("sub")
    is_site = grp >= regs
    has_low, has_high = sub > 0, sub < n_sub - 1
    source, part = grp // sites, grp % sites

    barrier = pltpu.get_barrier_semaphore()

    def greet(target):
        pl.semaphore_signal(barrier, inc=1, device_id=target, device_id_type=MESH)

    @pl.when(has_low)
    def _():
        greet((grp, sub - 1))

    @pl.when(has_high)
    def _():
        greet((grp, sub + 1))

    @pl.when(is_site)
    def _():
        for m in range(3):
            greet((m * sites + part, sub))

    def meet(others):
        peers = jnp.minimum(sub, 1) + jnp.minimum(n_sub - 1 - sub, 1) + others
        pl.semaphore_wait(barrier, peers)

    def halo(n, side):
        target = sub - 1 if side == 0 else sub + 1
        return pltpu.make_async_remote_copy(
            src_ref=send_ref.at[n, side],
            dst_ref=recv_ref.at[n, 1 - side],
            send_sem=halo_send.at[n, side],
            recv_sem=halo_recv.at[n, 1 - side],
            device_id=(grp, target),
            device_id_type=MESH,
        )

    def arrival(n, side):
        target = sub - 1 if side == 0 else sub + 1
        return pltpu.make_async_remote_copy(
            src_ref=send_ref.at[n, side],
            dst_ref=recv_ref.at[n, side],
            send_sem=halo_send.at[n, side],
            recv_sem=halo_recv.at[n, side],
            device_id=(grp, target),
            device_id_type=MESH,
        )

    def layer_copy(n, m):
        return pltpu.make_async_remote_copy(
            src_ref=layer_send_ref.at[n],
            dst_ref=layer_recv_ref.at[n, m],
            send_sem=layer_send.at[n],
            recv_sem=layer_recv.at[n, m],
            device_id=(regs + part, sub),
            device_id_type=MESH,
        )

    send_ref[...] = jnp.zeros_like(send_ref)

    @pl.when(jnp.logical_not(has_low))
    def _():
        recv_ref[:, 0] = jnp.zeros((STEPS, 8, slots), F32)

    @pl.when(jnp.logical_not(has_high))
    def _():
        recv_ref[:, 1] = jnp.zeros((STEPS, 8, slots), F32)

    lane = lax.broadcasted_iota(jnp.int32, (1, slots), 1)

    def exchange_start(n, force, send_map, first_fill, hp):
        for side in range(2):
            fill = slot_fill[0, :, first_fill + side : first_fill + side + 1]
            index = send_map[side : side + 1, :]
            blocks = jnp.where(lane < fill, index >> 7, -1)
            rows = pick(force, index & (LANES - 1), blocks, hp)
            for c in range(3):
                send_ref[n, side, c : c + 1, :] = rows[c]

        @pl.when(has_low)
        def _():
            halo(n, 0).start()

        @pl.when(has_high)
        def _():
            halo(n, 1).start()

    def exchange_end(n, recv_map, hot, hp):
        @pl.when(has_low)
        def _():
            arrival(n, 0).wait_recv()

        @pl.when(has_high)
        def _():
            arrival(n, 1).wait_recv()

        left = [
            spread_block(recv_ref[n, side], recv_map[side : side + 1, :] >> 7, hp) for side in range(2)
        ]
        total = dot(jnp.concatenate(left, axis=1), hot)
        return total[0 : 3 * hp] + total[3 * hp :]

    def step_on(s, force):
        u_ref, prev_ref, minv_ref = s[9], s[10], s[11]
        now = u_ref[...]
        later = 2.0 * now - prev_ref[...] + minv_ref[...] * force
        prev_ref[...] = now
        u_ref[...] = later
        return later

    def finish(d, s, out):
        for c in range(3):
            for h in range(d["h"]):
                at = c * d["hp"] + h
                out[c : c + 1, h * LANES : (h + 1) * LANES] = s[9][at : at + 1, :]

    def drain():
        def body(n, carry):
            @pl.when(has_low)
            def _():
                halo(n, 0).wait_send()

            @pl.when(has_high)
            def _():
                halo(n, 1).wait_send()

            return carry

        lax.fori_loop(0, STEPS, body, 0)

    @pl.when(jnp.logical_not(is_site))
    def _():
        site_out[...] = jnp.zeros_like(site_out)
        layer_send_ref[...] = jnp.zeros_like(layer_send_ref)
        prepare(rd, rs, reg_disp, reg_vel, reg_nodes, reg_coefs, reg_table, reg_minv, [reg_recv[...]], square, tmp)
        meet(1)
        hp = rd["hp"]

        def body(n, carry):
            force = element_forces(rd, rs)
            exchange_start(n, force, reg_send, 0, hp)
            force = force + exchange_end(n, reg_recv, rs[3][...], hp)
            later = step_on(rs, force)
            index = layer_src[0]
            blocks = jnp.where(lane < layer_fill[...], index >> 7, -1)
            rows = pick(later, index & (LANES - 1), blocks, hp)
            for c in range(3):
                layer_send_ref[n, c : c + 1, :] = rows[c]
            layer_copy(n, source).start()
            return carry

        lax.fori_loop(0, STEPS, body, 0)
        finish(rd, rs, reg_out)
        drain()

        def last(n, carry):
            layer_copy(n, source).wait_send()
            return carry

        lax.fori_loop(0, STEPS, last, 0)

    @pl.when(is_site)
    def _():
        reg_out[...] = jnp.zeros_like(reg_out)
        prepare(
            sd, ss, site_disp, site_vel, site_nodes, site_coefs, site_table, site_minv,
            [site_recv[...], layer_dst[...]], square, tmp,
        )
        meet(0)
        hp = sd["hp"]

        def body(n, carry):
            force = element_forces(sd, ss)
            exchange_start(n, force, site_send, 2, hp)
            for m in range(3):
                layer_copy(n, m).wait_recv()
            left = [
                spread_block(
                    layer_recv_ref[n, m] * layer_stiff[m : m + 1, :], layer_dst[m : m + 1, :] >> 7, hp
                )
                for m in range(3)
            ]
            total = dot(jnp.concatenate(left, axis=1), ss[3][2 * slots :, :])
            force = force + total[0 : 3 * hp] + total[3 * hp :]
            force = force + exchange_end(n, site_recv, ss[3][0 : 2 * slots, :], hp)
            step_on(ss, force)
            return carry

        lax.fori_loop(0, STEPS, body, 0)
        finish(sd, ss, site_out)
        drain()


def solution(mesh):
    n_grp, n_sub = mesh.shape["grp"], mesh.shape["sub"]

    def shards(*args):
        args = list(args)
        for k in (0, 1, 2, 3, 4, 5, 12, 13, 14, 15, 19, 20):
            args[k] = args[k].reshape(args[k].shape[2:])
        for k in (6, 7):
            args[k] = args[k].reshape((9,) + args[k].shape[4:])
        rd = sizes(args[4].shape, args[6].shape, args[0].shape)
        sd = sizes(args[5].shape, args[7].shape, args[2].shape)
        slots = args[12].shape[1]
        vmem = pl.BlockSpec(memory_space=pltpu.VMEM)
        reg_out, site_out = pl.pallas_call(
            functools.partial(kernel, n_grp, n_sub, rd, sd),
            out_shape=(
                jax.ShapeDtypeStruct(args[0].shape, F32),
                jax.ShapeDtypeStruct(args[2].shape, F32),
            ),
            in_specs=[vmem] * len(args),
            out_specs=(vmem, vmem),
            scratch_shapes=[
                pltpu.VMEM((STEPS, 2, 8, slots), F32),
                pltpu.VMEM((STEPS, 2, 8, slots), F32),
                pltpu.VMEM((STEPS, 8, slots), F32),
                pltpu.VMEM((STEPS, 3, 8, slots), F32),
                pltpu.VMEM((LANES, LANES), F32),
                pltpu.VMEM((LANES, slots), F32),
                pltpu.SemaphoreType.DMA((STEPS, 2)),
                pltpu.SemaphoreType.DMA((STEPS, 2)),
                pltpu.SemaphoreType.DMA((STEPS,)),
                pltpu.SemaphoreType.DMA((STEPS, 3)),
            ]
            + role_scratch(rd, 2)
            + role_scratch(sd, 5),
            compiler_params=pltpu.CompilerParams(
                collective_id=0, has_side_effects=True, vmem_limit_bytes=32 * 1024 * 1024
            ),
        )(*args)
        return reg_out[None, None], site_out[None, None]

    cell = ("grp", "sub")
    specs = [P(*cell)] * 21
    specs[8] = specs[9] = P()
    return jax.shard_map(
        shards,
        mesh=mesh,
        in_specs=tuple(specs),
        out_specs=(P(*cell), P(*cell)),
        check_vma=False,
    )
```

time: 603 us -> 42 us (0.07); the launches traced: 591 us -> 41.6 us
  other arithmetic: 351 us -> 0 us
  local copies, waits for them, and re-layouts: 139 us -> 5.51 us
  starting transfers between devices: 60.9 us -> 0 us
  Pallas kernels: 0 us -> 34.6 us
  waiting for transfers between devices: 24.9 us -> 0 us
    scatter-add x48 -> x0, other arithmetic: 288 us -> none  [the longest x8 205 us: stiff_force(): jnp.zeros_like(displaced).at[:, flat_nodes]]
    gather x24 -> x0, local copies, waits for them, and re-layouts: 91.5 us -> none  [the longest x8 73.9 us: stiff_force(): jnp.take(displaced, flat_nodes, axis=1).reshape(3, node_count, elem_count)]
    ppermute x32 -> x0, starting transfers between devices: 60.9 us -> none  [the longest x10 23.4 us: with_halo(): before = lax.ppermute(last, axis, up)]
    select_n x51 -> x0, other arithmetic: 39.6 us -> none  [the longest x16 30.3 us: stiff_force(): jnp.take(displaced, flat_nodes, axis=1).reshape(3, node_count, elem_count)]
    pallas_call x0 -> x1, Pallas kernels: none -> 34.6 us  [shards(): pl.pallas_call(functools.partial(kernel, n_grp, n_sub, rd, sd), out_shape...]
    ppermute x32 -> x0, waiting for transfers between devices: 24.9 us -> none  [the longest x10 21.6 us: with_halo(): after = lax.ppermute(leading, axis, down)]
    reshape x16 -> x0, local copies, waits for them, and re-layouts: 24.2 us -> none  [the longest x8 16.8 us: stiff_force(): element_terms.reshape(3, -1)]
    another operation x20 -> x0, other arithmetic: 10.1 us -> none  [the longest x8 5.4 us: shards(): layer_steps = jnp.stack(layer_packs)]
  transfers between devices with their start and end apart: 32 -> 0, of which waited for: 13 -> 0; matrix products, arithmetic and copies ran while one was open for 33% -> 0% of each run, Pallas kernels for 0% -> 0%
where the time goes in v1:
time: 42 us; the launch traced here: 41.6 us
  Pallas kernels  34.6 us (82%)
  local copies, waits for them, and re-layouts  5.51 us (13%)
  between operations  1.46 us (3%)
    pallas_call x1, Pallas kernels, shards(): pl.pallas_call(functools.partial(kernel, n_grp, n_sub, rd, sd), out_shape...  34.6 us
    unnamed x43, local copies, waits for them, and re-layouts  5.51 us

profile of v1, /device:TPU:23, one launch (start us, length us, event | category | flops | bytes accessed | tf_op | source)
XLA Modules:
  0.0 41.6 jit_solution(14681904836359792647)
XLA Ops:
  0.6 0.0 copy-start.16
  1.3 0.0 copy-start.14
  1.3 0.0 copy-start.15
  1.3 0.0 copy-start.13
  1.3 0.7 %copy-done.15 = s32[1,1,3,128]{3,1,2,0:T(1,128)S(1)} copy-done((s32[1,1,3,128]{3,1,2,0:T(1,128)S(1)}, s32[1,1,3,128]{3,1,2,0:T(1,128)}, u32[]{:S(2)}) %copy-start.15) | copy-done | bytes 1560
  2.0 0.0 copy-done.16
  2.0 0.0 copy-done.14
  2.0 0.0 copy-start.11
  2.0 0.7 %copy_bitcast_fusion.4 = (f32[3,384]{1,0:T(4,128)S(1)}, f32[3,384]{1,0:T(4,128)S(1)}) fusion(f32[1,1,3,384]{3,1,2,0:T(1,128)S(1)} %copy-done.14, f32[1,1,3,384]{3,1,2,0:T(1,128)} %param.21), kind=kLoop, calls=%fused_computation.4 | loop fusion | bytes 18432
  2.7 0.7 %copy.43 = s32[1,1,10,256]{3,2,1,0:T(8,128)S(1)} copy(s32[1,1,10,256]{3,1,2,0:T(1,128)} %param.25) | data formatting | bytes 20480
  3.5 0.7 %copy.42 = s32[1,1,35,128]{3,2,1,0:T(8,128)S(1)} copy(s32[1,1,35,128]{3,1,2,0:T(1,128)} %param.26) | data formatting | bytes 35840
  4.2 0.0 copy-done.11
  4.2 0.1 copy.23.site_table
  4.3 0.0 copy-done.13
  4.3 0.6 %copy-done.12 = f32[1,1,3,1536]{3,1,2,0:T(1,128)S(1)} copy-done((f32[1,1,3,1536]{3,1,2,0:T(1,128)S(1)}, f32[1,1,3,1536]{3,1,2,0:T(1,128)}, u32[]{:S(2)}) %copy-start.12) | copy-done | bytes 18456
  4.9 0.0 copy-start.7
  4.9 0.0 copy-start.8
  4.9 0.0 copy-start.10
  5.0 0.0 copy-start.4
  5.0 0.0 copy-start.5
  5.0 0.0 copy-start.9
  5.0 0.0 copy-done
  5.0 0.7 %copy-done.1 = f32[1,1,3,3,4,256]{5,4,3,2,1,0:T(4,128)S(1)} copy-done((f32[1,1,3,3,4,256]{5,4,3,2,1,0:T(4,128)S(1)}, f32[1,1,3,3,4,256]{5,4,3,2,1,0:T(4,128)}, u32[]{:S(2)}) %copy-start.1) | copy-done | bytes 36888
  5.7 0.0 copy-done.2
  5.7 0.0 copy-done.3
  5.7 0.0 copy-done.6
  5.7 0.0 copy-done.7
  5.7 0.0 copy-done.8
  5.7 0.0 copy-done.10
  5.7 34.6 %shard_map.212 = (f32[3,384]{1,0:T(4,128)S(1)}, f32[3,1536]{1,0:T(4,128)S(1)}) custom-call(f32[3,384]{1,0:T(4,128)S(1)} %get-tuple-element.11.reg_disp, f32[3,384]{1,0:T(4,128)S(1)} %get-tuple-element.10.reg_vel, f32[3,1536]{1,0:T(4,128)S(1)} %get-tuple-element.9.site_disp, f32[3,1536]{1,0:T(4,128)S(1)} %get-tuple-element.8.site_vel, ...), custom_call_target="tpu_custom_call" | custom-call | tf_op jit(solution)/shard_map/pallas_call | solution.py:411
  40.4 0.6 %copy.24 = f32[1,1,3,384]{3,1,2,0:T(1,128)} copy(f32[1,1,3,384]{3,2,1,0:T(4,128)S(1)} %bitcast.35) | data formatting | bytes 9216
  41.0 0.6 %copy.25 = f32[1,1,3,1536]{3,1,2,0:T(1,128)} copy(f32[1,1,3,1536]{3,2,1,0:T(4,128)S(1)} %bitcast.32) | data formatting | bytes 36864
  (12 shorter events, 0.0 us)
Async XLA Ops:
  0.6 1.4 %copy-start.16 = (f32[1,1,3,128]{3,1,2,0:T(1,128)S(1)}, f32[1,1,3,128]{3,1,2,0:T(1,128)}, u32[]{:S(2)}) copy-start(f32[1,1,3,128]{3,1,2,0:T(1,128)} %param.41) | copy-start | bytes 4612
  1.3 0.7 %copy-start.14 = (f32[1,1,3,384]{3,1,2,0:T(1,128)S(1)}, f32[1,1,3,384]{3,1,2,0:T(1,128)}, u32[]{:S(2)}) copy-start(f32[1,1,3,384]{3,1,2,0:T(1,128)} %param.22) | copy-start | bytes 13828
  1.3 0.7 %copy-start.15 = (s32[1,1,3,128]{3,1,2,0:T(1,128)S(1)}, s32[1,1,3,128]{3,1,2,0:T(1,128)}, u32[]{:S(2)}) copy-start(s32[1,1,3,128]{3,1,2,0:T(1,128)} %param.40) | copy-start | bytes 4612
  1.3 3.0 %copy-start.13 = (f32[1,1,3,1536]{3,1,2,0:T(1,128)S(1)}, f32[1,1,3,1536]{3,1,2,0:T(1,128)}, u32[]{:S(2)}) copy-start(f32[1,1,3,1536]{3,1,2,0:T(1,128)} %param.23) | copy-start | bytes 55300
  2.0 2.2 %copy-start.11 = (f32[72,35]{0,1:T(8,128)S(1)}, f32[72,35]{0,1:T(8,128)}, u32[]{:S(2)}) copy-start(f32[72,35]{0,1:T(8,128)} %param.30) | copy-start | bytes 30244
  2.7 2.3 %copy-start = (f32[1,1,3,3,24,128]{5,4,3,2,1,0:T(8,128)S(1)}, f32[1,1,3,3,24,128]{5,4,3,2,1,0:T(8,128)}, u32[]{:S(2)}) copy-start(f32[1,1,3,3,24,128]{5,4,3,2,1,0:T(8,128)} %param.28) | copy-start | bytes 331780
  4.2 0.7 %copy-start.12 = (f32[1,1,3,1536]{3,1,2,0:T(1,128)S(1)}, f32[1,1,3,1536]{3,1,2,0:T(1,128)}, u32[]{:S(2)}) copy-start(f32[1,1,3,1536]{3,1,2,0:T(1,128)} %param.24) | copy-start | bytes 55300
  4.9 0.8 %copy-start.1 = (f32[1,1,3,3,4,256]{5,4,3,2,1,0:T(4,128)S(1)}, f32[1,1,3,3,4,256]{5,4,3,2,1,0:T(4,128)}, u32[]{:S(2)}) copy-start(f32[1,1,3,3,4,256]{5,4,3,2,1,0:T(4,128)} %param.27) | copy-start | bytes 110596
  4.9 0.8 %copy-start.2 = (f32[12,10]{1,0:T(8,128)S(1)}, f32[12,10]{1,0:T(8,128)}, u32[]{:S(2)}) copy-start(f32[12,10]{1,0:T(8,128)} %reg_table.1) | copy-start | bytes 1444
  4.9 0.8 %copy-start.3 = (f32[1,1,1536]{2,1,0:T(1,128)S(1)}, f32[1,1,1536]{2,1,0:T(1,128)}, u32[]{:S(2)}) copy-start(f32[1,1,1536]{2,1,0:T(1,128)} %site_minv.1) | copy-start | bytes 18436
  4.9 0.8 %copy-start.6 = (s32[1,1,2,128]{3,2,1,0:T(2,128)S(1)}, s32[1,1,2,128]{3,2,1,0:T(2,128)}, u32[]{:S(2)}) copy-start(s32[1,1,2,128]{3,2,1,0:T(2,128)} %param.34) | copy-start | bytes 3076
  4.9 0.8 %copy-start.7 = (s32[1,1,2,128]{3,2,1,0:T(2,128)S(1)}, s32[1,1,2,128]{3,2,1,0:T(2,128)}, u32[]{:S(2)}) copy-start(s32[1,1,2,128]{3,2,1,0:T(2,128)} %param.35) | copy-start | bytes 3076
  4.9 0.8 %copy-start.8 = (s32[1,1,2,128]{3,2,1,0:T(2,128)S(1)}, s32[1,1,2,128]{3,2,1,0:T(2,128)}, u32[]{:S(2)}) copy-start(s32[1,1,2,128]{3,2,1,0:T(2,128)} %param.36) | copy-start | bytes 3076
  4.9 0.8 %copy-start.10 = (s32[1,1,128]{2,1,0:T(1,128)S(1)}, s32[1,1,128]{2,1,0:T(1,128)}, u32[]{:S(2)}) copy-start(s32[1,1,128]{2,1,0:T(1,128)} %layer_src.1) | copy-start | bytes 1540
  5.0 0.7 %copy-start.4 = (f32[1,1,384]{2,1,0:T(1,128)S(1)}, f32[1,1,384]{2,1,0:T(1,128)}, u32[]{:S(2)}) copy-start(f32[1,1,384]{2,1,0:T(1,128)} %reg_minv.1) | copy-start | bytes 4612
  5.0 0.7 %copy-start.5 = (s32[1,1,2,128]{3,2,1,0:T(2,128)S(1)}, s32[1,1,2,128]{3,2,1,0:T(2,128)}, u32[]{:S(2)}) copy-start(s32[1,1,2,128]{3,2,1,0:T(2,128)} %param.33) | copy-start | bytes 3076
  5.0 0.7 %copy-start.9 = (s32[1,1,4]{2,1,0:T(1,128)S(1)}, s32[1,1,4]{2,1,0:T(1,128)}, u32[]{:S(2)}) copy-start(s32[1,1,4]{2,1,0:T(1,128)} %slot_fill.1) | copy-start | bytes 52

commit v2 on v1

--- a/solution.py
+++ b/solution.py
@@ -59,9 +59,10 @@
 
 
 def fill_onehot(out_ref, first_row, lanes_index, tmp_ref):
-    count, length = lanes_index.shape
+    count, length = len(lanes_index), lanes_index[0].shape[1]
     tmp_ref[...] = jnp.zeros_like(tmp_ref)
-    tmp_ref[0:count, :] = lanes_index.astype(F32)
+    for r, row in enumerate(lanes_index):
+        tmp_ref[r : r + 1, :] = row.astype(F32)
     columns = tmp_ref[...].T
     lane = lax.broadcasted_iota(jnp.int32, (length, LANES), 1).astype(F32)
     for r in range(count):
@@ -81,7 +82,7 @@
 
 
 def sizes(nodes_shape, coefs_shape, disp_shape):
-    p, e = nodes_shape
+    p, _, e = nodes_shape
     q = coefs_shape[-2]
     h = disp_shape[-1] // LANES
     qp = up(q, 8)
@@ -111,35 +112,44 @@
     p, q, qp, kp, pp, hp = d["p"], d["q"], d["qp"], d["kp"], d["pp"], d["hp"]
     lane_ref[...] = jnp.zeros_like(lane_ref)
     block_ref[...] = jnp.full_like(block_ref, -1)
-    lane_ref[0:p, :] = nodes[...] & (LANES - 1)
-    block_ref[0:p, :] = nodes[...] >> 7
-    fill_onehot(hot_ref, 0, nodes[...] & (LANES - 1), tp)
-    row = 0
-    for index in slot_rows:
-        fill_onehot(slot_hot_ref, row, index & (LANES - 1), tmp)
-        row += index.shape[0] * index.shape[1]
+    for r in range(p):
+        lane_ref[r : r + 1, :] = nodes[r] & (LANES - 1)
+        block_ref[r : r + 1, :] = nodes[r] >> 7
+    fill_onehot(hot_ref, 0, [nodes[r] & (LANES - 1) for r in range(p)], tp)
+    fill_onehot(slot_hot_ref, 0, [row & (LANES - 1) for row in slot_rows], tmp)
     if qp != q:
         coef_ref[...] = jnp.zeros_like(coef_ref)
     coef_ref[:, 0:q, :] = coefs[...]
     square[...] = jnp.zeros_like(square)
+    turned_table = table.shape[0] == p
     for b in range(3):
-        square[b * qp : b * qp + q, 0:p] = table[b * q : (b + 1) * q, :]
-    high, low = split(square[0:kp, 0:pp])
-    dd_ref[0:kp, :] = high
-    dd_ref[kp : 2 * kp, :] = low
-    turned = square[...].T
-    square[...] = -turned
-    high, low = split(square[0:pp, 0:kp])
-    dt_ref[0:pp, :] = high
-    dt_ref[pp : 2 * pp, :] = low
+        if turned_table:
+            square[0:p, b * qp : b * qp + q] = table[:, b * q : (b + 1) * q]
+        else:
+            square[b * qp : b * qp + q, 0:p] = table[b * q : (b + 1) * q, :]
+
+    def plain():
+        high, low = split(square[0:kp, 0:pp])
+        dd_ref[0:kp, :] = high
+        dd_ref[kp : 2 * kp, :] = low
+
+    def turned():
+        high, low = split(-square[0:pp, 0:kp])
+        dt_ref[0:pp, :] = high
+        dt_ref[pp : 2 * pp, :] = low
+
+    first, second = (turned, plain) if turned_table else (plain, turned)
+    first()
+    square[...] = square[...].T
+    second()
     for ref in (u_ref, prev_ref, minv_ref):
         ref[...] = jnp.zeros_like(ref)
     for c in range(3):
         for h in range(d["h"]):
             at, cut = c * hp + h, slice(h * LANES, (h + 1) * LANES)
-            now = disp[c : c + 1, cut]
+            now = disp[c, :, cut]
             u_ref[at : at + 1, :] = now
-            prev_ref[at : at + 1, :] = now - vel[c : c + 1, cut]
+            prev_ref[at : at + 1, :] = now - vel[c, :, cut]
             minv_ref[at : at + 1, :] = minv[0, :, cut]
 
 
@@ -316,7 +326,7 @@
         for c in range(3):
             for h in range(d["h"]):
                 at = c * d["hp"] + h
-                out[c : c + 1, h * LANES : (h + 1) * LANES] = s[9][at : at + 1, :]
+                out[c, :, h * LANES : (h + 1) * LANES] = s[9][at : at + 1, :]
 
     def drain():
         def body(n, carry):
@@ -336,7 +346,7 @@
     def _():
         site_out[...] = jnp.zeros_like(site_out)
         layer_send_ref[...] = jnp.zeros_like(layer_send_ref)
-        prepare(rd, rs, reg_disp, reg_vel, reg_nodes, reg_coefs, reg_table, reg_minv, [reg_recv[...]], square, tmp)
+        prepare(rd, rs, reg_disp, reg_vel, reg_nodes, reg_coefs, reg_table, reg_minv, [reg_recv[k : k + 1, :] for k in range(2)], square, tmp)
         meet(1)
         hp = rd["hp"]
 
@@ -368,7 +378,7 @@
         reg_out[...] = jnp.zeros_like(reg_out)
         prepare(
             sd, ss, site_disp, site_vel, site_nodes, site_coefs, site_table, site_minv,
-            [site_recv[...], layer_dst[...]], square, tmp,
+            [site_recv[k : k + 1, :] for k in range(2)] + [layer_dst[m] for m in range(3)], square, tmp,
         )
         meet(0)
         hp = sd["hp"]
@@ -380,7 +390,7 @@
                 layer_copy(n, m).wait_recv()
             left = [
                 spread_block(
-                    layer_recv_ref[n, m] * layer_stiff[m : m + 1, :], layer_dst[m : m + 1, :] >> 7, hp
+                    layer_recv_ref[n, m] * layer_stiff[m], layer_dst[m] >> 7, hp
                 )
                 for m in range(3)
             ]
@@ -400,8 +410,12 @@
 
     def shards(*args):
         args = list(args)
-        for k in (0, 1, 2, 3, 4, 5, 12, 13, 14, 15, 19, 20):
+        for k in (0, 1, 2, 3, 4, 5, 19, 20):
+            rows, length = args[k].shape[2:]
+            args[k] = jnp.transpose(args[k], (0, 2, 1, 3)).reshape(rows, 1, length)
+        for k in (12, 13, 14, 15):
             args[k] = args[k].reshape(args[k].shape[2:])
+        args[9] = args[9].T
         for k in (6, 7):
             args[k] = args[k].reshape((9,) + args[k].shape[4:])
         rd = sizes(args[4].shape, args[6].shape, args[0].shape)
@@ -431,10 +445,10 @@
             + role_scratch(rd, 2)
             + role_scratch(sd, 5),
             compiler_params=pltpu.CompilerParams(
-                collective_id=0, has_side_effects=True, vmem_limit_bytes=32 * 1024 * 1024
+                collective_id=0, has_side_effects=True
             ),
         )(*args)
-        return reg_out[None, None], site_out[None, None]
+        return tuple(out.reshape(1, 1, out.shape[0], out.shape[2]) for out in (reg_out, site_out))
 
     cell = ("grp", "sub")
     specs = [P(*cell)] * 21

time: 42 us -> 40.3 us (0.960)
  local copies, waits for them, and re-layouts: 5.51 us -> 2.6 us
  Pallas kernels: 34.6 us -> 36.1 us
    unnamed x43 -> x4, local copies, waits for them, and re-layouts: 5.51 us -> 2.6 us
    pallas_call x1, Pallas kernels: 34.6 us -> 36.1 us  [shards(): pl.pallas_call(functools.partial(kernel, n_grp, n_sub, rd, sd), out_shape...]
where the time goes in v2:
time: 40.3 us; the launch traced here: 40.1 us
  Pallas kernels  36.1 us (90%)
  local copies, waits for them, and re-layouts  2.6 us (6%)
  between operations  1.3 us (3%)
    pallas_call x1, Pallas kernels, shards(): pl.pallas_call(functools.partial(kernel, n_grp, n_sub, rd, sd), out_shape...  36.1 us
    unnamed x4, local copies, waits for them, and re-layouts  2.6 us

profile of v2, /device:TPU:23, one launch (start us, length us, event | category | flops | bytes accessed | tf_op | source)
XLA Modules:
  0.0 40.1 jit_solution(9977000801379480816)
XLA Ops:
  1.3 36.1 %shard_map.212 = (f32[3,1,384]{2,1,0:T(1,128)}, f32[3,1,1536]{2,1,0:T(1,128)}) custom-call(f32[3,1,384]{2,1,0:T(1,128)} %bitcast.30, f32[3,1,384]{2,1,0:T(1,128)} %bitcast.31, f32[3,1,1536]{2,1,0:T(1,128)} %bitcast.24, f32[3,1,1536]{2,1,0:T(1,128)} %bitcast.25, s32[10,1,256]{2,1,0:T(1,128)} %bitcast.28, s32[35,1,128]{2,1,0:T(1,128)} %bitcast.27, ...), custom_call_target="tpu_custom_call" | custom-call | tf_op jit(solution)/shard_map/pallas_call | solution.py:425
  37.4 0.0 copy-start
  37.4 0.7 %copy-done = f32[3,1,384]{2,1,0:T(1,128)S(1)} copy-done((f32[3,1,384]{2,1,0:T(1,128)S(1)}, f32[3,1,384]{2,1,0:T(1,128)}, u32[]{:S(2)}) %copy-start) | copy-done | bytes 4632
  38.1 0.6 %copy.28 = f32[1,1,3,384]{3,1,2,0:T(1,128)} copy(f32[1,1,3,384]{3,1,2,0:T(1,128)S(1)} %bitcast.29) | data formatting | bytes 9216
  38.7 1.3 %copy.29 = f32[1,1,3,1536]{3,1,2,0:T(1,128)} copy(f32[1,1,3,1536]{3,1,2,0:T(1,128)} %bitcast.26) | data formatting | bytes 36864
Async XLA Ops:
  37.4 0.7 %copy-start = (f32[3,1,384]{2,1,0:T(1,128)S(1)}, f32[3,1,384]{2,1,0:T(1,128)}, u32[]{:S(2)}) copy-start(f32[3,1,384]{2,1,0:T(1,128)} %get-tuple-element.4) | copy-start | bytes 13828
